TPU v7x, 32 devices: a whole 2x2x4 slice. The times are simulated.
32 devices in a mesh: row: 8 (over y, x, core), shift: 4 (over z).
Axes of the slice: x: 2, y: 2, z: 4, core: 2. Of those that a mesh axis runs over, the one named last changes fastest.
Arguments:
- snapshots: bfloat16 [4096, 2, 128], P('row'), may hold values from -6 to 6
- tail_sensors: bfloat16 [128, 2, 128], replicated, may hold values from -6 to 6
- shift_offsets: int32 [12], P('shift'), may hold values from 0 to 128
- start_basis: float32 [64, 4096], P(None, 'row'), may hold values from -0.09375 to 0.09375
Outputs:
- covariance: float32 [4096, 4096], P('row', 'shift')
- signal_basis: float32 [64, 4096], P(None, 'row')
Inputs may be any that keep to these rules, and one draw needn't show every extreme that they name: `shift_offsets`: each shift's first sensor.
All inputs are finite; a program needn't handle non-finite values.
Results may differ from a plain program's by a relative error of at most 0.0031.
Values may be sent and summed in bfloat16 or wider, within the bound.
A program may use at most 64 MiB of HBM per device.

v0:
```python
import functools

import jax
import jax.numpy as jnp
from jax import lax
from jax.experimental import pallas as pl
from jax.experimental.pallas import tpu as pltpu
from jax.sharding import PartitionSpec as P

MESH = pl.DeviceIdType.MESH
HALF_ROOT = 0.7071067811865476
NT = (((1,), (1,)), ((), ()))
NN = (((1,), (0,)), ((), ()))
CHUNK = 128
GROUP = 8


def split(value):
    high = value.astype(jnp.bfloat16)
    return high, (value - high.astype(jnp.float32)).astype(jnp.bfloat16)


def dot(left, right, dims):
    return lax.dot_general(left, right, dims, preferred_element_type=jnp.float32)


def dot3(left, right, dims):
    left_high, left_low = split(left)
    right_high, right_low = split(right)
    return dot(left_high, right_high, dims) + (
        dot(left_low, right_high, dims) + dot(left_high, right_low, dims)
    )


def dot_full(left, right, dims):
    return lax.dot_general(
        left,
        right,
        dims,
        precision=lax.Precision.HIGHEST,
        preferred_element_type=jnp.float32,
    )


def inverse_factor(gram):
    k = gram.shape[0]
    row_ids = lax.broadcasted_iota(jnp.int32, (k, k), 0)
    col_ids = lax.broadcasted_iota(jnp.int32, (k, k), 1)
    eye = jnp.where(row_ids == col_ids, 1.0, 0.0).astype(jnp.float32)
    table = jnp.concatenate([gram, eye], axis=1)
    tall = lax.broadcasted_iota(jnp.int32, (k, 2 * k), 0)
    for j in range(0, k, GROUP):
        columns = [jnp.broadcast_to(table[:, j + a : j + a + 1], (k, 2 * k)) for a in range(GROUP)]
        rows = [table[j + a : j + a + 1, :] for a in range(GROUP)]
        for a in range(GROUP):
            inverse = 1.0 / columns[a][j + a : j + a + 1, :]
            scaled = rows[a] * inverse
            for c in range(a + 1, GROUP):
                shared = columns[a][j + c : j + c + 1, :]
                factor = columns[c][j + a : j + a + 1, :] * inverse
                columns[c] = columns[c] - columns[a] * factor
                rows[c] = rows[c] - scaled * shared
            table = table - jnp.where(tall > j + a, columns[a] * scaled, 0.0)
    pivots = jnp.sum(jnp.where(row_ids == col_ids, table[:, :k], 0.0), axis=1, keepdims=True)
    return table[:, k:] * lax.rsqrt(pivots)


def kernel(
    n_row, n_shift, m,
    snap_ref, tail_ref, offs_ref, start_ref,
    cov_ref, basis_ref,
    xb, xf, rf, prow, pcol, cov, offs_v, offs_s,
    t1, rs1, ag1, t2, rs2, ag2, g1, g2,
    x_send, x_fwd, x_recv, o_send, o_recv,
    rs1_send, rs1_recv, ag1_send, ag1_recv,
    rs2_send, rs2_recv, ag2_send, ag2_recv,
    g1_send, g1_recv, g2_send, g2_recv, local_sem, cov_sem,
):
    me = lax.axis_index("row")
    col = lax.axis_index("shift")
    rows = snap_ref.shape[0]
    tail = tail_ref.shape[0]
    k = start_ref.shape[0]
    cols = m // n_shift
    pair = me % 2
    mate = me + 1 - 2 * pair

    barrier = pltpu.get_barrier_semaphore()
    for d in range(1, n_row):
        pl.semaphore_signal(barrier, inc=1, device_id={"row": (me + d) % n_row}, device_id_type=MESH)
    for d in range(1, n_shift):
        pl.semaphore_signal(barrier, inc=1, device_id={"shift": (col + d) % n_shift}, device_id_type=MESH)
    pl.semaphore_wait(barrier, n_row + n_shift - 2)

    sends = []

    def remote(src, dst, send, recv, axis, index):
        return pltpu.make_async_remote_copy(
            src_ref=src, dst_ref=dst, send_sem=send, recv_sem=recv,
            device_id={axis: index}, device_id_type=MESH,
        )

    def push(*args):
        copy = remote(*args)
        copy.start()
        sends.append(copy)

    def block(index):
        return xb.at[pl.ds(pl.multiple_of(index * rows, rows), rows)]

    lanes_of = lax.broadcasted_iota(jnp.int32, (1, 128), 1)
    listed = jnp.zeros((1, 128), jnp.int32)
    for j in range(offs_ref.shape[0]):
        listed = jnp.where(lanes_of == j, offs_ref[j], listed)
    offs_v[col] = listed

    for d in range(1, n_shift):
        push(offs_v.at[col], offs_v.at[col], o_send.at[d], o_recv.at[col], "shift", (col + d) % n_shift)
    for d in range(1, n_row // 2):
        push(snap_ref, block(me), x_send.at[d], x_recv.at[me], "row", (me + 2 * d) % n_row)
    push(snap_ref, block(me), x_send.at[0], x_recv.at[me], "row", mate)
    own_copy = pltpu.make_async_copy(snap_ref, block(me), local_sem.at[0])
    own_copy.start()
    tail_copy = pltpu.make_async_copy(tail_ref, xb.at[pl.ds(m, tail)], local_sem.at[1])
    tail_copy.start()

    flip_rows = lax.broadcasted_iota(jnp.int32, (CHUNK, CHUNK), 0)
    flip_cols = lax.broadcasted_iota(jnp.int32, (CHUNK, CHUNK), 1)
    flip = jnp.where(flip_rows + flip_cols == CHUNK - 1, 1.0, 0.0).astype(jnp.bfloat16)

    def spread(first, count):
        def one(c, carry):
            at = pl.multiple_of(first + c * CHUNK, CHUNK)
            value = xb[pl.ds(at, CHUNK), :]
            plain = value.astype(jnp.float32)
            back = dot(flip, value, NN)
            other = pl.multiple_of(m + tail - CHUNK - at, CHUNK)
            half = plain.shape[1] // 2
            xf[0, pl.ds(at, CHUNK), :] = plain[:, :half]
            xf[1, pl.ds(at, CHUNK), :] = plain[:, half:]
            rf[0, pl.ds(other, CHUNK), :] = back[:, :half]
            rf[1, pl.ds(other, CHUNK), :] = back[:, half:]
            return carry

        lax.fori_loop(0, count // CHUNK, one, 0)

    tail_copy.wait()
    spread(m, tail)
    own_copy.wait()
    for d in range(n_row // 2):
        src = (me + n_row - 2 * d) % n_row
        if d:
            remote(snap_ref, block(src), x_send.at[d], x_recv.at[src], "row", src).wait_recv()
            push(block(src), block(src), x_fwd.at[d], x_recv.at[src], "row", mate)
        spread(src * rows, rows)
    for d in range(n_row // 2):
        src = (mate + n_row - 2 * d) % n_row
        remote(snap_ref, block(src), x_send.at[d], x_recv.at[src], "row", mate).wait_recv()
        spread(src * rows, rows)

    for d in range(1, n_shift):
        src = (col + n_shift - d) % n_shift
        remote(offs_v.at[src], offs_v.at[src], o_send.at[d], o_recv.at[src], "shift", src).wait_recv()
    to_scalar = pltpu.make_async_copy(offs_v, offs_s, local_sem.at[2])
    to_scalar.start()
    to_scalar.wait()

    snaps = xf.shape[2]
    width = 2 * snaps
    per = prow.shape[1] // (width * n_shift)

    def fill(target, start, count):
        lower = start >= m // 2
        first = jnp.where(lower, 1, 0)
        second = 1 - first
        sign = jnp.where(lower, -1.0, 1.0).astype(jnp.float32)

        def one_shift(s, carry):
            offset = offs_s[s // per, 0, s % per]
            lanes = pl.multiple_of(s * width, width)
            for c in range(count // CHUNK):
                near = pl.ds(offset + start + c * CHUNK, CHUNK)
                far = pl.ds(tail - offset + start + c * CHUNK, CHUNK)
                left = (xf[first, near, :] + sign * rf[first, far, :]) * HALF_ROOT
                right = (xf[second, near, :] + sign * rf[second, far, :]) * (sign * HALF_ROOT)
                target[pl.ds(c * CHUNK, CHUNK), pl.ds(lanes, snaps)] = left.astype(jnp.bfloat16)
                target[pl.ds(c * CHUNK, CHUNK), pl.ds(pl.multiple_of(lanes + snaps, snaps), snaps)] = right.astype(jnp.bfloat16)
            return carry

        lax.fori_loop(0, per * n_shift, one_shift, 0)

    fill(prow, me * rows, rows)
    fill(pcol, col * cols, cols)

    normalizer = 1.0 / (snaps * per * n_shift)
    tile = 256

    def one_tile(c, carry):
        at = pl.multiple_of(c * tile, tile)
        cov[:, pl.ds(at, tile)] = dot(prow[...], pcol[pl.ds(at, tile), :], NT) * normalizer
        return carry

    lax.fori_loop(0, cols // tile, one_tile, 0)
    cov_copy = pltpu.make_async_copy(cov, cov_ref, cov_sem)
    cov_copy.start()

    def scatter(value, out, landing, send, recv, axis, index, n):
        piece = k // n
        for p in range(n):
            out[p] = value[p * piece : (p + 1) * piece, :]
        for d in range(1, n):
            p = (index + d) % n
            push(out.at[p], landing.at[index], send.at[d], recv.at[index], axis, p)

    def collect(out, landing, held, send, recv, send2, recv2, axis, index, n):
        for d in range(1, n):
            p = (index + n - d) % n
            remote(out.at[p], landing.at[p], send.at[d], recv.at[p], axis, p).wait_recv()
        landing[index] = out[index]
        total = landing[0]
        for p in range(1, n):
            total = total + landing[p]
        held[index] = total
        for d in range(1, n):
            p = (index + d) % n
            push(held.at[index], held.at[index], send2.at[d], recv2.at[index], axis, p)

    def arrive(held, send, recv, axis, index, n):
        for d in range(1, n):
            p = (index + n - d) % n
            remote(held.at[p], held.at[p], send.at[d], recv.at[p], axis, p).wait_recv()

    def whole(held, n):
        return jnp.concatenate([held[p] for p in range(n)], axis=0)

    scatter(dot3(start_ref[...], cov[...], NN), t1, rs1, rs1_send, rs1_recv, "row", me, n_row)
    collect(t1, rs1, ag1, rs1_send, rs1_recv, ag1_send, ag1_recv, "row", me, n_row)
    arrive(ag1, ag1_send, ag1_recv, "row", me, n_row)
    mapped = whole(ag1, n_row)

    g1[col] = dot_full(mapped, mapped, NT)
    for d in range(1, n_shift):
        push(g1.at[col], g1.at[col], g1_send.at[d], g1_recv.at[col], "shift", (col + d) % n_shift)
    scatter(dot3(mapped, cov[...], NT), t2, rs2, rs2_send, rs2_recv, "shift", col, n_shift)
    arrive(g1, g1_send, g1_recv, "shift", col, n_shift)
    collect(t2, rs2, ag2, rs2_send, rs2_recv, ag2_send, ag2_recv, "shift", col, n_shift)
    gram = g1[0]
    for p in range(1, n_shift):
        gram = gram + g1[p]
    first_inverse = inverse_factor(gram)
    arrive(ag2, ag2_send, ag2_recv, "shift", col, n_shift)
    mapped = dot_full(first_inverse, whole(ag2, n_shift), NN)

    g2[me] = dot_full(mapped, mapped, NT)
    for d in range(1, n_row):
        push(g2.at[me], g2.at[me], g2_send.at[d], g2_recv.at[me], "row", (me + d) % n_row)
    arrive(g2, g2_send, g2_recv, "row", me, n_row)
    gram = g2[0]
    for p in range(1, n_row):
        gram = gram + g2[p]
    basis_ref[...] = dot_full(inverse_factor(gram), mapped, NN)

    for copy in sends:
        copy.wait_send()
    cov_copy.wait()


def per_device(n_row, n_shift, m, snapshots, tail_sensors, shift_offsets, start_basis):
    rows = snapshots.shape[0]
    tail = tail_sensors.shape[0]
    k = start_basis.shape[0]
    cols = m // n_shift
    per = shift_offsets.shape[0]
    width = snapshots.shape[1] * snapshots.shape[2]
    vmem = pl.BlockSpec(memory_space=pltpu.VMEM)
    f32, bf16 = jnp.float32, jnp.bfloat16
    dma = pltpu.SemaphoreType.DMA
    return pl.pallas_call(
        functools.partial(kernel, n_row, n_shift, m),
        out_shape=(
            jax.ShapeDtypeStruct((rows, cols), f32),
            jax.ShapeDtypeStruct((k, rows), f32),
        ),
        in_specs=[vmem, vmem, pl.BlockSpec(memory_space=pltpu.SMEM), vmem],
        out_specs=(pl.BlockSpec(memory_space=pl.ANY), vmem),
        scratch_shapes=[
            pltpu.VMEM((m + tail, width), bf16),
            pltpu.VMEM((2, m + tail, width // 2), f32),
            pltpu.VMEM((2, m + tail, width // 2), f32),
            pltpu.VMEM((rows, width * per * n_shift), bf16),
            pltpu.VMEM((cols, width * per * n_shift), bf16),
            pltpu.VMEM((rows, cols), f32),
            pltpu.VMEM((n_shift, 1, 128), jnp.int32),
            pltpu.SMEM((n_shift, 1, 128), jnp.int32),
            pltpu.VMEM((n_row, k // n_row, cols), f32),
            pltpu.VMEM((n_row, k // n_row, cols), f32),
            pltpu.VMEM((n_row, k // n_row, cols), f32),
            pltpu.VMEM((n_shift, k // n_shift, rows), f32),
            pltpu.VMEM((n_shift, k // n_shift, rows), f32),
            pltpu.VMEM((n_shift, k // n_shift, rows), f32),
            pltpu.VMEM((n_shift, k, k), f32),
            pltpu.VMEM((n_row, k, k), f32),
            dma((n_row,)), dma((n_row,)), dma((n_row,)),
            dma((n_shift,)), dma((n_shift,)),
            dma((n_row,)), dma((n_row,)), dma((n_row,)), dma((n_row,)),
            dma((n_shift,)), dma((n_shift,)), dma((n_shift,)), dma((n_shift,)),
            dma((n_shift,)), dma((n_shift,)), dma((n_row,)), dma((n_row,)),
            dma((3,)), dma,
        ],
        compiler_params=pltpu.CompilerParams(
            collective_id=0, has_side_effects=True, vmem_limit_bytes=32 * 1024 * 1024
        ),
    )(snapshots.reshape(rows, width), tail_sensors.reshape(tail, width), shift_offsets, start_basis)


def solution(mesh):
    n_row, n_shift = mesh.shape["row"], mesh.shape["shift"]

    def step(snapshots, tail_sensors, shift_offsets, start_basis):
        m = snapshots.shape[0]
        return jax.shard_map(
            functools.partial(per_device, n_row, n_shift, m),
            mesh=mesh,
            in_specs=(P("row", None, None), P(), P("shift"), P(None, "row")),
            out_specs=(P("row", "shift"), P(None, "row")),
            check_vma=False,
        )(snapshots, tail_sensors, shift_offsets, start_basis)

    return step
```

profile of v0, /device:TPU:0, one launch (start us, length us, event | category | flops | bytes accessed | tf_op | source)
XLA Modules:
  0.0 65.8 jit_solution(18334728994014136869)
XLA Ops:
  0.6 0.9 %copy.11 = bf16[16,8,2,128]{3,1,2,0:T(8,128)(2,1)S(1)} copy(bf16[16,8,2,128]{3,2,1,0:T(2,128)(2,1)} %bitcast.11) | data formatting | bytes 131072
  1.5 1.0 %copy.10 = bf16[64,8,2,128]{3,1,2,0:T(8,128)(2,1)S(1)} copy(bf16[64,8,2,128]{3,2,1,0:T(2,128)(2,1)} %bitcast.10) | data formatting | bytes 524288
  2.5 0.0 copy-start
  2.5 0.9 %copy-done = f32[64,512]{1,0:T(8,128)S(1)} copy-done((f32[64,512]{1,0:T(8,128)S(1)}, f32[64,512]{1,0:T(8,128)}, u32[]{:S(2)}) %copy-start) | copy-done | bytes 131096
  3.4 0.0 copy-start.1
  3.4 0.7 copy-done.1
  4.0 59.7 %shard_map.59 = (f32[512,1024]{1,0:T(8,128)S(1)}, f32[64,512]{1,0:T(8,128)S(1)}) custom-call(bf16[512,256]{1,0:T(8,128)(2,1)S(1)} %bitcast.8, bf16[128,256]{1,0:T(8,128)(2,1)S(1)} %bitcast.9, s32[3]{0:T(128)S(1)} %copy-done.1, f32[64,512]{1,0:T(8,128)S(1)} %copy-done), custom_call_target="tpu_custom_call" | custom-call | tf_op jit(solution)/shard_map/pallas_call | solution.py:278
  63.8 1.3 %copy.14 = f32[512,1024]{1,0:T(8,128)} copy(f32[512,1024]{1,0:T(8,128)S(1)} %get-tuple-element.4) | data formatting | bytes 4194304
  65.1 0.7 copy.15
Async XLA Ops:
  2.5 0.9 %copy-start = (f32[64,512]{1,0:T(8,128)S(1)}, f32[64,512]{1,0:T(8,128)}, u32[]{:S(2)}) copy-start(f32[64,512]{1,0:T(8,128)} %start_ref.1) | copy-start | bytes 393220
  3.4 0.7 copy-start.1
where the time goes:
time: 66 us; the launch traced here: 65.8 us
  Pallas kernels  59.7 us (90%)
  local copies, waits for them, and re-layouts  5.37 us (8%)
    pallas_call x1, Pallas kernels, per_device(): pl.pallas_call(functools.partial(kernel, n_row, n_shift, m), out_shape=(j...  59.7 us
    unnamed x8, local copies, waits for them, and re-layouts  5.37 us

commit v1 on v0

--- a/solution.py
+++ b/solution.py
@@ -71,7 +71,7 @@
     cov_ref, basis_ref,
     xb, xf, rf, prow, pcol, cov, offs_v, offs_s,
     t1, rs1, ag1, t2, rs2, ag2, g1, g2,
-    x_send, x_fwd, x_recv, o_send, o_recv,
+    x_send, x_recv, o_send, o_recv,
     rs1_send, rs1_recv, ag1_send, ag1_recv,
     rs2_send, rs2_recv, ag2_send, ag2_recv,
     g1_send, g1_recv, g2_send, g2_recv, local_sem, cov_sem,
@@ -116,9 +116,37 @@
 
     for d in range(1, n_shift):
         push(offs_v.at[col], offs_v.at[col], o_send.at[d], o_recv.at[col], "shift", (col + d) % n_shift)
-    for d in range(1, n_row // 2):
-        push(snap_ref, block(me), x_send.at[d], x_recv.at[me], "row", (me + 2 * d) % n_row)
-    push(snap_ref, block(me), x_send.at[0], x_recv.at[me], "row", mate)
+    half_rows = rows // 2
+
+    def part(index, h):
+        return xb.at[pl.ds(pl.multiple_of(index * rows + h * half_rows, half_rows), half_rows)]
+
+    def own_part(h):
+        return snap_ref.at[pl.ds(h * half_rows, half_rows)]
+
+    used = []
+
+    def give(src, index, h, peer):
+        push(src, part(index, h), x_send.at[len(used)], x_recv.at[2 * index + h], "row", peer)
+        used.append(1)
+
+    def take(index, h):
+        remote(own_part(h), part(index, h), x_send.at[0], x_recv.at[2 * index + h], "row", mate).wait_recv()
+
+    square = n_row == 8
+    if square:
+        quarter = me // 2
+        along = 2 * (quarter + 1 - 2 * (quarter % 2)) + pair
+        across = 2 * (quarter + 2 - 4 * (quarter // 2)) + pair
+        opposite = 2 * (3 - quarter) + pair
+        for h, peer in ((0, along), (1, across), (1, along), (0, across)):
+            give(own_part(h), me, h, peer)
+    else:
+        for d in range(1, n_row // 2):
+            for h in range(2):
+                give(own_part(h), me, h, (me + 2 * d) % n_row)
+    for h in range(2):
+        give(own_part(h), me, h, mate)
     own_copy = pltpu.make_async_copy(snap_ref, block(me), local_sem.at[0])
     own_copy.start()
     tail_copy = pltpu.make_async_copy(tail_ref, xb.at[pl.ds(m, tail)], local_sem.at[1])
@@ -147,16 +175,35 @@
     tail_copy.wait()
     spread(m, tail)
     own_copy.wait()
-    for d in range(n_row // 2):
-        src = (me + n_row - 2 * d) % n_row
-        if d:
-            remote(snap_ref, block(src), x_send.at[d], x_recv.at[src], "row", src).wait_recv()
-            push(block(src), block(src), x_fwd.at[d], x_recv.at[src], "row", mate)
-        spread(src * rows, rows)
-    for d in range(n_row // 2):
-        src = (mate + n_row - 2 * d) % n_row
-        remote(snap_ref, block(src), x_send.at[d], x_recv.at[src], "row", mate).wait_recv()
-        spread(src * rows, rows)
+    spread(me * rows, rows)
+
+    def swap(index):
+        return index + 1 - 2 * (index % 2)
+
+    if square:
+        for index, h, onward in (
+            (along, 0, across), (across, 1, along), (along, 1, None),
+            (across, 0, None), (opposite, 0, None), (opposite, 1, None),
+        ):
+            take(index, h)
+            if onward is not None:
+                give(part(index, h), index, h, onward)
+            give(part(index, h), index, h, mate)
+            if index is not opposite and onward is None:
+                spread(index * rows, rows)
+        spread(opposite * rows, rows)
+        others = [along, across, opposite]
+    else:
+        others = [(me + n_row - 2 * d) % n_row for d in range(1, n_row // 2)]
+        for index in others:
+            for h in range(2):
+                take(index, h)
+                give(part(index, h), index, h, mate)
+            spread(index * rows, rows)
+    for index in [me] + others:
+        for h in range(2):
+            take(swap(index), h)
+        spread(swap(index) * rows, rows)
 
     for d in range(1, n_shift):
         src = (col + n_shift - d) % n_shift
@@ -193,17 +240,6 @@
     fill(pcol, col * cols, cols)
 
     normalizer = 1.0 / (snaps * per * n_shift)
-    tile = 256
-
-    def one_tile(c, carry):
-        at = pl.multiple_of(c * tile, tile)
-        cov[:, pl.ds(at, tile)] = dot(prow[...], pcol[pl.ds(at, tile), :], NT) * normalizer
-        return carry
-
-    lax.fori_loop(0, cols // tile, one_tile, 0)
-    cov_copy = pltpu.make_async_copy(cov, cov_ref, cov_sem)
-    cov_copy.start()
-
     def scatter(value, out, landing, send, recv, axis, index, n):
         piece = k // n
         for p in range(n):
@@ -233,10 +269,32 @@
     def whole(held, n):
         return jnp.concatenate([held[p] for p in range(n)], axis=0)
 
-    scatter(dot3(start_ref[...], cov[...], NN), t1, rs1, rs1_send, rs1_recv, "row", me, n_row)
-    collect(t1, rs1, ag1, rs1_send, rs1_recv, ag1_send, ag1_recv, "row", me, n_row)
-    arrive(ag1, ag1_send, ag1_recv, "row", me, n_row)
-    mapped = whole(ag1, n_row)
+    tiles = t1.shape[0]
+    tile = cols // tiles
+
+    def settle(c):
+        collect(
+            t1.at[c], rs1.at[c], ag1.at[c], rs1_send.at[c], rs1_recv.at[c],
+            ag1_send.at[c], ag1_recv.at[c], "row", me, n_row,
+        )
+
+    start = start_ref[...]
+    for c in range(tiles):
+        at = pl.ds(c * tile, tile)
+        cov[:, at] = dot(prow[...], pcol[at, :], NT) * normalizer
+        scatter(
+            dot3(start, cov[:, at], NN), t1.at[c], rs1.at[c],
+            rs1_send.at[c], rs1_recv.at[c], "row", me, n_row,
+        )
+        if c >= 2:
+            settle(c - 2)
+    cov_copy = pltpu.make_async_copy(cov, cov_ref, cov_sem)
+    cov_copy.start()
+    for c in range(max(tiles - 2, 0), tiles):
+        settle(c)
+    for c in range(tiles):
+        arrive(ag1.at[c], ag1_send.at[c], ag1_recv.at[c], "row", me, n_row)
+    mapped = jnp.concatenate([whole(ag1.at[c], n_row) for c in range(tiles)], axis=1)
 
     g1[col] = dot_full(mapped, mapped, NT)
     for d in range(1, n_shift):
@@ -272,6 +330,7 @@
     cols = m // n_shift
     per = shift_offsets.shape[0]
     width = snapshots.shape[1] * snapshots.shape[2]
+    tiles = max(cols // 256, 1)
     vmem = pl.BlockSpec(memory_space=pltpu.VMEM)
     f32, bf16 = jnp.float32, jnp.bfloat16
     dma = pltpu.SemaphoreType.DMA
@@ -292,17 +351,17 @@
             pltpu.VMEM((rows, cols), f32),
             pltpu.VMEM((n_shift, 1, 128), jnp.int32),
             pltpu.SMEM((n_shift, 1, 128), jnp.int32),
-            pltpu.VMEM((n_row, k // n_row, cols), f32),
-            pltpu.VMEM((n_row, k // n_row, cols), f32),
-            pltpu.VMEM((n_row, k // n_row, cols), f32),
+            pltpu.VMEM((tiles, n_row, k // n_row, cols // tiles), f32),
+            pltpu.VMEM((tiles, n_row, k // n_row, cols // tiles), f32),
+            pltpu.VMEM((tiles, n_row, k // n_row, cols // tiles), f32),
             pltpu.VMEM((n_shift, k // n_shift, rows), f32),
             pltpu.VMEM((n_shift, k // n_shift, rows), f32),
             pltpu.VMEM((n_shift, k // n_shift, rows), f32),
             pltpu.VMEM((n_shift, k, k), f32),
             pltpu.VMEM((n_row, k, k), f32),
-            dma((n_row,)), dma((n_row,)), dma((n_row,)),
+            dma((2 * n_row,)), dma((2 * n_row,)),
             dma((n_shift,)), dma((n_shift,)),
-            dma((n_row,)), dma((n_row,)), dma((n_row,)), dma((n_row,)),
+            dma((tiles, n_row)), dma((tiles, n_row)), dma((tiles, n_row)), dma((tiles, n_row)),
             dma((n_shift,)), dma((n_shift,)), dma((n_shift,)), dma((n_shift,)),
             dma((n_shift,)), dma((n_shift,)), dma((n_row,)), dma((n_row,)),
             dma((3,)), dma,

time: 66 us -> 65.1 us (0.986)
  Pallas kernels: 59.7 us -> 58.8 us
    pallas_call x1, Pallas kernels: 59.7 us -> 58.8 us  [per_device(): pl.pallas_call(functools.partial(kernel, n_row, n_shift, m), out_shape=(j...]
where the time goes in v1:
time: 65.1 us; the launch traced here: 64.8 us
  Pallas kernels  58.8 us (90%)
  local copies, waits for them, and re-layouts  5.37 us (8%)
    pallas_call x1, Pallas kernels, per_device(): pl.pallas_call(functools.partial(kernel, n_row, n_shift, m), out_shape=(j...  58.8 us
    unnamed x8, local copies, waits for them, and re-layouts  5.37 us

profile of v1, /device:TPU:0, one launch (start us, length us, event | category | flops | bytes accessed | tf_op | source)
XLA Modules:
  0.0 64.8 jit_solution(9246498477868755513)
XLA Ops:
  0.6 0.9 %copy.11 = bf16[16,8,2,128]{3,1,2,0:T(8,128)(2,1)S(1)} copy(bf16[16,8,2,128]{3,2,1,0:T(2,128)(2,1)} %bitcast.11) | data formatting | bytes 131072
  1.5 1.0 %copy.10 = bf16[64,8,2,128]{3,1,2,0:T(8,128)(2,1)S(1)} copy(bf16[64,8,2,128]{3,2,1,0:T(2,128)(2,1)} %bitcast.10) | data formatting | bytes 524288
  2.5 0.0 copy-start
  2.5 0.9 %copy-done = f32[64,512]{1,0:T(8,128)S(1)} copy-done((f32[64,512]{1,0:T(8,128)S(1)}, f32[64,512]{1,0:T(8,128)}, u32[]{:S(2)}) %copy-start) | copy-done | bytes 131096
  3.4 0.0 copy-start.1
  3.4 0.7 %copy-done.1 = s32[3]{0:T(128)S(1)} copy-done((s32[3]{0:T(128)S(1)}, s32[3]{0:T(128)}, u32[]{:S(2)}) %copy-start.1) | copy-done | bytes 36
  4.0 58.8 %shard_map.59 = (f32[512,1024]{1,0:T(8,128)S(1)}, f32[64,512]{1,0:T(8,128)S(1)}) custom-call(bf16[512,256]{1,0:T(8,128)(2,1)S(1)} %bitcast.8, bf16[128,256]{1,0:T(8,128)(2,1)S(1)} %bitcast.9, s32[3]{0:T(128)S(1)} %copy-done.1, f32[64,512]{1,0:T(8,128)S(1)} %copy-done), custom_call_target="tpu_custom_call" | custom-call | tf_op jit(solution)/shard_map/pallas_call | solution.py:337
  62.9 1.3 %copy.14 = f32[512,1024]{1,0:T(8,128)} copy(f32[512,1024]{1,0:T(8,128)S(1)} %get-tuple-element.4) | data formatting | bytes 4194304
  64.2 0.7 %copy.15 = f32[64,512]{1,0:T(8,128)} copy(f32[64,512]{1,0:T(8,128)S(1)} %get-tuple-element.5) | data formatting | bytes 262144
Async XLA Ops:
  2.5 0.9 %copy-start = (f32[64,512]{1,0:T(8,128)S(1)}, f32[64,512]{1,0:T(8,128)}, u32[]{:S(2)}) copy-start(f32[64,512]{1,0:T(8,128)} %start_ref.1) | copy-start | bytes 393220
  3.4 0.7 %copy-start.1 = (s32[3]{0:T(128)S(1)}, s32[3]{0:T(128)}, u32[]{:S(2)}) copy-start(s32[3]{0:T(128)} %offs_ref.1) | copy-start | bytes 40
